TPU v7x, 32 devices: a whole 2x2x4 slice. The times are simulated.
32 devices in a mesh: grp: 4 (over y, x), row: 8 (over z, core).
Axes of the slice: x: 2, y: 2, z: 4, core: 2. Of those that a mesh axis runs over, the one named last changes fastest.
Arguments:
- krylov_basis: bfloat16 [300, 512, 512], P(None, 'row', 'grp'), may hold values from -30 to 30
- krylov_image: bfloat16 [300, 512, 512], P(None, 'row', 'grp'), may hold values from -30 to 30
- tridiag_vectors: bfloat16 [300, 32], P(None, 'grp'), may hold values from -0.375 to 0.375
- ritz_values: bfloat16 [32], P('grp'), may hold values from -3 to 3
Outputs:
- ritz_vectors: float32 [32, 512, 512], P('grp', 'row')
- ritz_residuals: float32 [32, 512, 512], P('grp', 'row')
- residual_norms: float32 [32], P('grp')
All inputs are finite; a program needn't handle non-finite values.
Results may differ from a plain program's by a relative error of at most 0.0003.
Values may be sent and summed in bfloat16 or wider, within the bound.
A program may use at most 64 MiB of HBM per device.

v0:
```python
import jax
import jax.numpy as jnp
from jax import lax
from jax.sharding import PartitionSpec as P


def project(coef_cols, field_block):
    krylov_len = field_block.shape[0]
    flat_field = field_block.reshape(krylov_len, -1)
    result = lax.dot_general(
        coef_cols, flat_field, (((0,), (0,)), ((), ())), preferred_element_type=jnp.float32
    )
    return result.reshape(coef_cols.shape[1], field_block.shape[1], field_block.shape[2])


def column_pair(coef_cols, shift_values, basis_block, image_block):
    ritz_cols = project(coef_cols, basis_block)
    applied = project(coef_cols, image_block)
    resid_cols = applied - shift_values[:, None, None] * ritz_cols
    return (ritz_cols, resid_cols)


def squares_of(ritz_cols, resid_cols):
    return (
        jnp.sum(ritz_cols * ritz_cols, axis=(1, 2)),
        jnp.sum(resid_cols * resid_cols, axis=(1, 2)),
    )


def finish(ritz_cols, resid_cols, ritz_squares, resid_squares, rows_total):
    ritz_squares = ritz_squares + 1.0
    factor = jnp.sqrt(rows_total / ritz_squares)
    return (
        ritz_cols * factor[:, None, None],
        resid_cols * factor[:, None, None],
        jnp.sqrt(resid_squares / ritz_squares),
    )


def body(krylov_basis, krylov_image, tridiag_vectors, ritz_values):
    groups = lax.axis_size("grp")
    outer_dev = krylov_basis.shape[1]
    inner_dev = krylov_basis.shape[2]
    rows_total = float(outer_dev * inner_dev * groups * lax.axis_size("row"))
    all_coefs, all_values = (
        lax.all_gather(tridiag_vectors, "grp", axis=1, tiled=True),
        lax.all_gather(ritz_values, "grp", axis=0, tiled=True),
    )
    ritz_cols, resid_cols = column_pair(
        all_coefs, all_values.astype(jnp.float32), krylov_basis, krylov_image
    )
    owned_ritz, owned_resid = (
        lax.all_to_all(ritz_cols, "grp", split_axis=0, concat_axis=2, tiled=True),
        lax.all_to_all(resid_cols, "grp", split_axis=0, concat_axis=2, tiled=True),
    )
    ritz_part, resid_part = squares_of(owned_ritz, owned_resid)
    ritz_squares, resid_squares = lax.psum((ritz_part, resid_part), "row")
    return finish(owned_ritz, owned_resid, ritz_squares, resid_squares, rows_total)


def solution(mesh):
    placed = (P(None, "row", "grp"), P(None, "row", "grp"), P(None, "grp"), P("grp"))
    return jax.shard_map(
        body,
        mesh=mesh,
        in_specs=placed,
        out_specs=(P("grp", "row", None), P("grp", "row", None), P("grp")),
        check_vma=False,
    )
```

profile of v0, /device:TPU:0, one launch (start us, length us, event | category | flops | bytes accessed | tf_op | source)
XLA Modules:
  0.0 82.6 jit_solution(6580176041747844001)
XLA Ops:
  0.6 0.0 copy-start.1
  0.6 6.0 %slice_bitcast_fusion.1 = bf16[64,128,300]{1,0,2:T(8,128)(2,1)} fusion(bf16[300,64,128]{2,1,0:T(8,128)(2,1)} %param.4), kind=kLoop, calls=%fused_computation.5 | loop fusion | bytes 9830400 | tf_op jit(solution)/shard_map/dot_general | solution.py:10
  6.6 0.0 copy-done.1
  6.6 0.0 copy-start.4
  6.6 0.0 copy-start.3
  6.6 0.0 copy-start.2
  6.6 3.3 %slice_bitcast_fusion = bf16[64,128,300]{1,0,2:T(8,128)(2,1)} fusion(bf16[300,64,128]{2,1,0:T(8,128)(2,1)S(1)} %copy-done.1), kind=kLoop, calls=%fused_computation.4 | loop fusion | bytes 9830400 | tf_op jit(solution)/shard_map/dot_general | solution.py:10
  10.0 0.0 copy-done.4
  10.0 0.6 dynamic-slice
  11.2 0.0 copy-done.3
  11.2 0.2 dynamic-update-slice
  11.5 0.0 copy-done.2
  11.5 9.7 %all_gather.6 = bf16[300,32]{0,1:T(8,128)(2,1)S(1)} all-gather(bf16[300,8]{0,1:T(8,128)(2,1)S(1)} %copy-done.2), channel_id=1, replica_groups=mesh['grp'=4,'row'=8] {'grp'}, dimensions={1}, use_global_device_ids=true | all-gather | bytes 24000 | tf_op jit(solution)/shard_map/all_gather | solution.py:46
  21.1 8.9 %all-reduce = bf16[32]{0:T(256)(128)(2,1)S(1)} all-reduce(bf16[32]{0:T(256)(128)(2,1)S(1)} %dynamic-update-slice), channel_id=1, replica_groups=mesh['grp'=4,'row'=8] {'grp'}, use_global_device_ids=true, to_apply=%add | all-reduce | flops 32 | bytes 128
  30.1 0.0 copy-start
  30.1 5.6 %fusion.2 = f32[32,64,128]{2,0,1:T(8,128)S(1)} fusion(bf16[64,128,300]{1,0,2:T(8,128)(2,1)} %slice_bitcast_fusion.1, bf16[300,32]{0,1:T(8,128)(2,1)S(1)} %all_gather.6), kind=kOutput, calls=%fused_computation.2 | convolution fusion | flops 157286400 | bytes 5982976 | tf_op jit(solution)/shard_map/dot_general | solution.py:10
  35.7 0.0 copy-done
  35.7 3.1 %fusion.4 = f32[32,64,128]{2,0,1:T(8,128)S(1)} fusion(bf16[64,128,300]{1,0,2:T(8,128)(2,1)S(1)} %copy-done, f32[32,64,128]{2,0,1:T(8,128)S(1)} %fusion.2, f32[32]{0:T(128)S(1)} %convert_element_type.3, bf16[300,32]{0,1:T(8,128)(2,1)S(1)} %all_gather.6), kind=kOutput, calls=%fused_computation.6 | convolution fusion | flops 157810688 | bytes 7031680 | tf_op jit(solution)/shard_map/dot_general | solution.py:10
  38.7 1.6 %copy.17 = f32[32,64,128]{2,1,0:T(8,128)} copy(f32[32,64,128]{2,0,1:T(8,128)S(1)} %fusion.4) | data formatting | bytes 2097152 | tf_op jit(solution)/shard_map/sub | solution.py:19
  40.3 3.5 %all-to-all-start.1 = ((f32[32,64,128]{2,1,0:T(8,128)}), f32[32,64,128]{2,1,0:T(8,128)S(1)}, u32[]{:S(2)}, u32[]{:S(2)}) async-start(f32[32,64,128]{2,1,0:T(8,128)} %copy.17), calls=%async_computation.1 | async-start | bytes 2097152 | tf_op jit(solution)/shard_map/all_to_all | solution.py:54
  43.8 1.6 %copy.14 = f32[32,64,128]{2,1,0:T(8,128)} copy(f32[32,64,128]{2,0,1:T(8,128)S(1)} %fusion.2) | data formatting | bytes 2097152 | tf_op jit(solution)/shard_map/dot_general | solution.py:10
  45.4 8.3 %all-to-all-done.1 = f32[32,64,128]{2,1,0:T(8,128)S(1)} async-done(((f32[32,64,128]{2,1,0:T(8,128)}), f32[32,64,128]{2,1,0:T(8,128)S(1)}, u32[]{:S(2)}, u32[]{:S(2)}) %all-to-all-start.1) | async-done | bytes 1048608 | tf_op jit(solution)/shard_map/all_to_all | solution.py:54
  53.7 3.5 %all-to-all-start = ((f32[32,64,128]{2,1,0:T(8,128)}), f32[32,64,128]{2,1,0:T(8,128)S(1)}, u32[]{:S(2)}, u32[]{:S(2)}) async-start(f32[32,64,128]{2,1,0:T(8,128)} %copy.14), calls=%async_computation | async-start | bytes 2097152 | tf_op jit(solution)/shard_map/all_to_all | solution.py:53
  57.3 0.2 multiply_reduce_fusion
  57.4 9.2 %all-to-all-done = f32[32,64,128]{2,1,0:T(8,128)S(1)} async-done(((f32[32,64,128]{2,1,0:T(8,128)}), f32[32,64,128]{2,1,0:T(8,128)S(1)}, u32[]{:S(2)}, u32[]{:S(2)}) %all-to-all-start) | async-done | bytes 1048608 | tf_op jit(solution)/shard_map/all_to_all | solution.py:53
  66.7 0.2 multiply_reduce_fusion.1
  66.8 13.6 %all-reduce.1 = (f32[8]{0:T(128)S(1)}, f32[8]{0:T(128)S(1)}) all-reduce(f32[8]{0:T(128)S(1)} %multiply_reduce_fusion.1, f32[8]{0:T(128)S(1)} %multiply_reduce_fusion), channel_id=1, replica_groups=mesh['grp'=4,'row'=8] {'row'}, use_global_device_ids=true, to_apply=%region_1.0 | all-reduce | flops 16 | bytes 128 | tf_op jit(solution)/shard_map/psum | solution.py:57
  80.4 0.5 divide_sqrt_fusion.1
  80.9 1.7 %bitcast_multiply_fusion = (f32[8,64,512]{2,1,0:T(8,128)}, f32[8,64,512]{2,1,0:T(8,128)}) fusion(f32[4,8,8,8,128]{4,3,2,1,0:T(8,128)S(1)} %bitcast.43, f32[8]{0:T(128)S(1)} %get-tuple-element.6, f32[4,8,8,8,128]{4,3,2,1,0:T(8,128)S(1)} %bitcast.45), kind=kLoop, calls=%fused_computation.7 | loop fusion | flops 524288 | bytes 4194336 | tf_op jit(solution)/shard_map/mul | solution.py:35
  (2 shorter events, 0.0 us)
Async XLA Ops:
  0.6 6.0 %copy-start.1 = (bf16[300,64,128]{2,1,0:T(8,128)(2,1)S(1)}, bf16[300,64,128]{2,1,0:T(8,128)(2,1)}, u32[]{:S(2)}) copy-start(bf16[300,64,128]{2,1,0:T(8,128)(2,1)} %param.5) | copy-start | bytes 14745604
  6.6 3.4 %copy-start.4 = (u32[32]{0:T(128)S(1)}, u32[32]{0:T(128)}, u32[]{:S(2)}) copy-start(u32[32]{0:T(128)} %constant.8) | copy-start | bytes 388
  6.6 4.6 %copy-start.3 = (bf16[8]{0:T(256)(128)(2,1)S(1)}, bf16[8]{0:T(256)(128)(2,1)}, u32[]{:S(2)}) copy-start(bf16[8]{0:T(256)(128)(2,1)} %param.7) | copy-start | bytes 52
  6.6 4.9 %copy-start.2 = (bf16[300,8]{0,1:T(8,128)(2,1)S(1)}, bf16[300,8]{0,1:T(8,128)(2,1)}, u32[]{:S(2)}) copy-start(bf16[300,8]{0,1:T(8,128)(2,1)} %param.6) | copy-start | bytes 14404
  30.1 5.6 %copy-start = (bf16[64,128,300]{1,0,2:T(8,128)(2,1)S(1)}, bf16[64,128,300]{1,0,2:T(8,128)(2,1)}, u32[]{:S(2)}) copy-start(bf16[64,128,300]{1,0,2:T(8,128)(2,1)} %slice_bitcast_fusion) | copy-start | bytes 14745604
  40.3 13.4 %all-to-all-start.1 = ((f32[32,64,128]{2,1,0:T(8,128)}), f32[32,64,128]{2,1,0:T(8,128)S(1)}, u32[]{:S(2)}, u32[]{:S(2)}) async-start(f32[32,64,128]{2,1,0:T(8,128)} %copy.17), calls=%async_computation.1 | async-start | bytes 2097152 | tf_op jit(solution)/shard_map/all_to_all | solution.py:54
  53.7 12.9 %all-to-all-start = ((f32[32,64,128]{2,1,0:T(8,128)}), f32[32,64,128]{2,1,0:T(8,128)S(1)}, u32[]{:S(2)}, u32[]{:S(2)}) async-start(f32[32,64,128]{2,1,0:T(8,128)} %copy.14), calls=%async_computation | async-start | bytes 2097152 | tf_op jit(solution)/shard_map/all_to_all | solution.py:53
where the time goes:
time: 82.9 us; the launch traced here: 82.6 us
  blocking collectives  32.2 us (39%)
  waiting for transfers between devices  17.5 us (21%)
  local copies, waits for them, and re-layouts  13.3 us (16%)
  matrix products  8.63 us (10%)
  starting transfers between devices  7.04 us (8%)
  other arithmetic  2.56 us (3%)
  between operations  1.37 us (2%)
    psum x1, blocking collectives, body(): ritz_squares, resid_squares = lax.psum((ritz_part, resid_part), 'row')  13.6 us
    dot_general x3, local copies, waits for them, and re-layouts, project(): lax.dot_general(coef_cols, flat_field, (((0,), (0,)), ((), ())), preferre...  10.9 us
    all_gather x1, blocking collectives, body(): lax.all_gather(tridiag_vectors, 'grp', axis=1, tiled=True)  9.66 us
    all_to_all x1, waiting for transfers between devices, body(): lax.all_to_all(ritz_cols, 'grp', split_axis=0, concat_axis=2, tiled=True)  9.22 us
    unnamed x1, blocking collectives  8.95 us
    dot_general x2, matrix products, project(): lax.dot_general(coef_cols, flat_field, (((0,), (0,)), ((), ())), preferre...  8.63 us
    all_to_all x1, waiting for transfers between devices, body(): lax.all_to_all(resid_cols, 'grp', split_axis=0, concat_axis=2, tiled=True)  8.3 us
    all_to_all x1, starting transfers between devices, body(): lax.all_to_all(ritz_cols, 'grp', split_axis=0, concat_axis=2, tiled=True)  3.52 us
  transfers between devices with their start and end apart: 2, of which 2 were waited for; matrix products, arithmetic and copies ran while one was open for 2% of the time, Pallas kernels for 0%

commit v1 on v0

v1 whole, which is shorter than its diff:
```python
import functools
import math

import jax
import jax.numpy as jnp
from jax import lax
from jax.experimental import pallas as pl
from jax.experimental.pallas import tpu as pltpu
from jax.sharding import PartitionSpec as P

MESH = pl.DeviceIdType.MESH
TILE = 16
LANES = 128
SPREAD = 256.0
REACH = 86.0
SLOPE = 2.0 * REACH / math.log(1.0 + SPREAD)
LEAST = 1e-35


def cdiv(a, b):
    return (a + b - 1) // b


def grid_iota(shape, dim):
    return lax.broadcasted_iota(jnp.int32, shape, dim)


def expand_rows(cols, width):
    return jnp.broadcast_to(cols, (cols.shape[0], width)).reshape(cols.shape[0], 1, width)


def exchange_kernel(
    groups, rows, krylov_len,
    packed_ref, basis_ref, image_ref,
    coded_ref, stats_ref, total_ref,
    coefs, fields, spread, reps, expanded, coded, stat_send, stat_recv, row_send, row_recv,
    load_sem, coef_sems, data_sems, own_sem, stat_sems, row_sems,
):
    wanted_dev, packed_width = packed_ref.shape
    wanted = groups * wanted_dev
    chunks = fields.shape[1]
    inner_dev = basis_ref.shape[2]
    padded_len = fields.shape[2]
    steps = padded_len // TILE
    wide = TILE * TILE
    block = wanted_dev * TILE
    grp = lax.axis_index("grp")
    row = lax.axis_index("row")
    lane_stats = grid_iota((wanted, LANES), 1)

    def loads(chunk):
        span = pl.ds(pl.multiple_of(chunk * TILE, TILE), TILE)
        return [
            pltpu.make_async_copy(
                ref.at[:, span, :], fields.at[which, chunk, pl.ds(0, krylov_len)], load_sem.at[which, chunk]
            )
            for which, ref in enumerate((basis_ref, image_ref))
        ]

    for chunk in range(chunks):
        for copy in loads(chunk):
            copy.start()

    barrier = pltpu.get_barrier_semaphore()
    for step in range(1, groups):
        pl.semaphore_signal(barrier, inc=1, device_id={"grp": lax.rem(grp + step, groups)}, device_id_type=MESH)
    for step in range(1, rows):
        pl.semaphore_signal(barrier, inc=1, device_id={"row": lax.rem(row + step, rows)}, device_id_type=MESH)
    pl.semaphore_wait(barrier, groups + rows - 2)

    def remote(src, dst, sems, index, axis, step):
        me, size = (grp, groups) if axis == "grp" else (row, rows)
        return pltpu.make_async_remote_copy(
            src_ref=src,
            dst_ref=dst,
            send_sem=sems.at[(0,) + index],
            recv_sem=sems.at[(1,) + index],
            device_id={axis: lax.rem(me + step, size)},
            device_id_type=MESH,
        )

    def coef_copy(step):
        return remote(packed_ref, coefs.at[grp], coef_sems, (step,), "grp", step)

    for step in range(1, groups):
        coef_copy(step).start()
    coefs[grp] = packed_ref[...]

    if padded_len > krylov_len:
        for chunk in range(chunks):
            for which in range(2):
                fields[which, chunk, pl.ds(krylov_len, padded_len - krylov_len)] = jnp.zeros(
                    (padded_len - krylov_len, TILE, inner_dev), jnp.bfloat16
                )
    shape = spread.shape
    spread[...] = jnp.where(
        lax.shift_right_logical(grid_iota(shape, 1), 4) == grid_iota(shape, 0), 1.0, 0.0
    ).astype(jnp.bfloat16)

    for step in range(1, groups):
        coef_copy(step).wait()

    all_coefs = coefs[...].reshape(wanted, packed_width)
    shift_values = expand_rows(all_coefs[:, packed_width - 1 :], inner_dev)
    for part in range(cdiv(steps * TILE, LANES)):
        reps[part] = jnp.dot(
            all_coefs[:, part * LANES : (part + 1) * LANES].astype(jnp.bfloat16),
            spread[...],
            preferred_element_type=jnp.float32,
        )
    per_part = LANES // TILE
    same = (grid_iota((TILE, wide), 1) & (TILE - 1)) == grid_iota((TILE, wide), 0)
    for step in range(steps):
        at = (step % per_part) * wide
        values = reps[step // per_part, :, at : at + wide]
        values = jnp.where(same[None], values.reshape(wanted, 1, wide), 0.0)
        expanded[:, step * wide : (step + 1) * wide] = values.reshape(wanted * TILE, wide).astype(jnp.bfloat16)

    def data_copy(chunk, step):
        dest = lax.rem(grp + step, groups)
        return remote(
            coded.at[chunk, pl.ds(pl.multiple_of(dest * block, block), block)],
            coded_ref.at[grp, chunk],
            data_sems, (chunk, step), "grp", step,
        )

    def own_copy(chunk):
        return pltpu.make_async_copy(
            coded.at[chunk, pl.ds(pl.multiple_of(grp * block, block), block)],
            coded_ref.at[grp, chunk],
            own_sem.at[chunk],
        )

    def stat_copy(step):
        return remote(
            stat_send.at[lax.rem(grp + step, groups)], stat_recv.at[grp], stat_sems, (step,), "grp", step
        )

    def compute(chunk, stats):
        for copy in loads(chunk):
            copy.wait()
        both = jnp.concatenate(
            [fields[which, chunk].reshape(padded_len * TILE, inner_dev) for which in range(2)], axis=1
        )
        product = jnp.dot(expanded[...], both, preferred_element_type=jnp.float32)
        product = product.reshape(wanted, TILE, 2 * inner_dev)
        ritz = product[:, :, :inner_dev]
        resid = product[:, :, inner_dev:] - shift_values * ritz
        for kind, cols in enumerate((ritz, resid)):
            squares = jnp.sum(jnp.sum(cols * cols, axis=1), axis=1, keepdims=True)
            most = jnp.max(jnp.max(jnp.abs(cols), axis=1), axis=1, keepdims=True)
            most = jnp.maximum(most, LEAST)
            codes = jnp.exp(SLOPE * jnp.log(1.0 + jnp.abs(cols) * expand_rows(SPREAD / most, inner_dev)) - REACH)
            codes = jnp.where(cols < 0.0, -codes, codes)
            coded[chunk, :, kind * inner_dev : (kind + 1) * inner_dev] = codes.reshape(
                wanted * TILE, inner_dev
            ).astype(jnp.bfloat16)
            stats = jnp.where(lane_stats == 2 * chunk + kind, most, stats)
            stats = jnp.where(lane_stats == 2 * chunks + kind, stats + squares, stats)

        @pl.when(chunk == chunks - 1)
        def _():
            stat_send[...] = stats.reshape(groups, wanted_dev, LANES)
            for step in range(1, groups):
                stat_copy(step).start()

        for step in range(1, groups):
            data_copy(chunk, step).start()
        own_copy(chunk).start()
        return stats

    lax.fori_loop(0, chunks, compute, jnp.zeros((wanted, LANES), jnp.float32))

    for step in range(1, groups):
        stat_copy(step).wait()
    stat_recv[grp] = stat_send[grp]
    row_send[...] = jnp.sum(stat_recv[...], axis=0)

    def row_copy(step):
        return remote(row_send, row_recv.at[row], row_sems, (step,), "row", step)

    for step in range(1, rows):
        row_copy(step).start()
    stats_ref[...] = stat_recv[...]
    row_recv[row] = row_send[...]
    for step in range(1, rows):
        row_copy(step).wait()
    total_ref[...] = jnp.sum(row_recv[...], axis=0)

    def finish(chunk, carry):
        for step in range(1, groups):
            data_copy(chunk, step).wait()
        own_copy(chunk).wait()
        return carry

    lax.fori_loop(0, chunks, finish, 0)


def finish_kernel(rows_total, chunks, coded_ref, stats_ref, total_ref, ritz_ref, resid_ref, norm_ref):
    chunk = pl.program_id(0)
    groups, wanted_dev = stats_ref.shape[:2]
    inner_dev = coded_ref.shape[3] // 2
    lanes = grid_iota((wanted_dev, LANES), 1)

    def pick(tile, lane):
        return jnp.sum(jnp.where(lanes == lane, tile, 0.0), axis=1, keepdims=True)

    total = total_ref[...]
    ritz_squares = pick(total, 2 * chunks) + 1.0
    resid_squares = pick(total, 2 * chunks + 1)
    factor = jnp.sqrt(rows_total / ritz_squares)
    for source in range(groups):
        for kind, out_ref in enumerate((ritz_ref, resid_ref)):
            scale = pick(stats_ref[source], 2 * chunk + kind) * (factor * (1.0 / SPREAD))
            codes = coded_ref[source, 0, :, kind * inner_dev : (kind + 1) * inner_dev].astype(jnp.float32)
            size = jnp.exp((jnp.log(jnp.abs(codes)) + REACH) * (1.0 / SLOPE)) - 1.0
            size = jnp.where(codes < 0.0, -size, size)
            size = size.reshape(wanted_dev, TILE, inner_dev)
            out_ref[:, :, source * inner_dev : (source + 1) * inner_dev] = size * expand_rows(scale, inner_dev)
    norms = jnp.broadcast_to(jnp.sqrt(resid_squares / ritz_squares), (wanted_dev, LANES))
    diagonal = lanes == grid_iota((wanted_dev, LANES), 0)
    norm_ref[...] = jnp.sum(jnp.where(diagonal, norms, 0.0), axis=0, keepdims=True)


def body(groups, rows, krylov_basis, krylov_image, tridiag_vectors, ritz_values):
    krylov_len, outer_dev, inner_dev = krylov_basis.shape
    wanted_dev = tridiag_vectors.shape[1]
    wanted = groups * wanted_dev
    chunks = outer_dev // TILE
    block = wanted_dev * TILE
    padded_len = cdiv(krylov_len, TILE) * TILE
    packed_width = cdiv(padded_len + 1, LANES) * LANES
    rows_total = float(outer_dev * inner_dev * groups * rows)
    packed = jnp.concatenate(
        [
            tridiag_vectors.astype(jnp.float32).T,
            jnp.zeros((wanted_dev, packed_width - krylov_len - 1), jnp.float32),
            ritz_values.astype(jnp.float32)[:, None],
        ],
        axis=1,
    )
    f32, bf16 = jnp.float32, jnp.bfloat16
    dma = pltpu.SemaphoreType.DMA
    anywhere = pl.BlockSpec(memory_space=pl.ANY)
    vmem = pl.BlockSpec(memory_space=pltpu.VMEM)
    parts = cdiv(padded_len, LANES)
    coded, stats, total = pl.pallas_call(
        functools.partial(exchange_kernel, groups, rows, krylov_len),
        name="exchange",
        out_shape=(
            jax.ShapeDtypeStruct((groups, chunks, block, 2 * inner_dev), bf16),
            jax.ShapeDtypeStruct((groups, wanted_dev, LANES), f32),
            jax.ShapeDtypeStruct((wanted_dev, LANES), f32),
        ),
        in_specs=[vmem, anywhere, anywhere],
        out_specs=(anywhere, vmem, vmem),
        scratch_shapes=[
            pltpu.VMEM((groups, wanted_dev, packed_width), f32),
            pltpu.VMEM((2, chunks, padded_len, TILE, inner_dev), bf16),
            pltpu.VMEM((LANES, LANES * TILE), bf16),
            pltpu.VMEM((parts, wanted, LANES * TILE), f32),
            pltpu.VMEM((wanted * TILE, padded_len * TILE), bf16),
            pltpu.VMEM((chunks, wanted * TILE, 2 * inner_dev), bf16),
            pltpu.VMEM((groups, wanted_dev, LANES), f32),
            pltpu.VMEM((groups, wanted_dev, LANES), f32),
            pltpu.VMEM((wanted_dev, LANES), f32),
            pltpu.VMEM((rows, wanted_dev, LANES), f32),
            dma((2, chunks)),
            dma((2, groups)),
            dma((2, chunks, groups)),
            dma((chunks,)),
            dma((2, groups)),
            dma((2, rows)),
        ],
        compiler_params=pltpu.CompilerParams(
            collective_id=0, has_side_effects=True, vmem_limit_bytes=48 * 1024 * 1024
        ),
    )(packed, krylov_basis, krylov_image)
    ritz_vectors, ritz_residuals, norms = pl.pallas_call(
        functools.partial(finish_kernel, rows_total, chunks),
        name="finish",
        grid=(chunks,),
        out_shape=(
            jax.ShapeDtypeStruct((wanted_dev, outer_dev, groups * inner_dev), f32),
            jax.ShapeDtypeStruct((wanted_dev, outer_dev, groups * inner_dev), f32),
            jax.ShapeDtypeStruct((1, LANES), f32),
        ),
        in_specs=[
            pl.BlockSpec((groups, 1, block, 2 * inner_dev), lambda c: (0, c, 0, 0)),
            pl.BlockSpec((groups, wanted_dev, LANES), lambda c: (0, 0, 0)),
            pl.BlockSpec((wanted_dev, LANES), lambda c: (0, 0)),
        ],
        out_specs=(
            pl.BlockSpec((wanted_dev, TILE, groups * inner_dev), lambda c: (0, c, 0)),
            pl.BlockSpec((wanted_dev, TILE, groups * inner_dev), lambda c: (0, c, 0)),
            pl.BlockSpec((1, LANES), lambda c: (0, 0)),
        ),
    )(coded, stats, total)
    return ritz_vectors, ritz_residuals, norms[0, :wanted_dev]


def solution(mesh):
    placed = (P(None, "row", "grp"), P(None, "row", "grp"), P(None, "grp"), P("grp"))
    return jax.shard_map(
        functools.partial(body, mesh.shape["grp"], mesh.shape["row"]),
        mesh=mesh,
        in_specs=placed,
        out_specs=(P("grp", "row", None), P("grp", "row", None), P("grp")),
        check_vma=False,
    )
```

time: 82.9 us -> 40.5 us (0.49)
  Pallas kernels: 0 us -> 32.2 us
  blocking collectives: 32.2 us -> 0 us
  waiting for transfers between devices: 17.5 us -> 0 us
  matrix products: 8.63 us -> 0 us
  local copies, waits for them, and re-layouts: 13.3 us -> 5.89 us
  starting transfers between devices: 7.04 us -> 0 us
  other arithmetic: 2.56 us -> 1.43 us
    pallas_call x0 -> x2, Pallas kernels: none -> 32.2 us  [the longest x1 28.2 us: body(): pl.pallas_call(functools.partial(exchange_kernel, groups, rows, krylov_le...]
    all_to_all x2 -> x0, waiting for transfers between devices: 17.5 us -> none  [the longest x1 9.22 us: body(): lax.all_to_all(ritz_cols, 'grp', split_axis=0, concat_axis=2, tiled=True)]
    psum x1 -> x0, blocking collectives: 13.6 us -> none  [body(): ritz_squares, resid_squares = lax.psum((ritz_part, resid_part), 'row')]
    dot_general x3 -> x0, local copies, waits for them, and re-layouts: 10.9 us -> none  [project(): lax.dot_general(coef_cols, flat_field, (((0,), (0,)), ((), ())), preferre...]
    all_gather x1 -> x0, blocking collectives: 9.66 us -> none  [body(): lax.all_gather(tridiag_vectors, 'grp', axis=1, tiled=True)]
    unnamed x1 -> x0, blocking collectives: 8.95 us -> none
    dot_general x2 -> x0, matrix products: 8.63 us -> none  [project(): lax.dot_general(coef_cols, flat_field, (((0,), (0,)), ((), ())), preferre...]
    all_to_all x2 -> x0, starting transfers between devices: 7.04 us -> none  [the longest x1 3.52 us: body(): lax.all_to_all(ritz_cols, 'grp', split_axis=0, concat_axis=2, tiled=True)]
  transfers between devices with their start and end apart: 2 -> 0, of which waited for: 2 -> 0; matrix products, arithmetic and copies ran while one was open for 2% -> 0% of each run, Pallas kernels for 0% -> 0%
where the time goes in v1:
time: 40.5 us; the launch traced here: 40.2 us
  Pallas kernels  32.2 us (80%)
  local copies, waits for them, and re-layouts  5.89 us (15%)
  other arithmetic  1.43 us (4%)
  between operations  0.65 us (2%)
    pallas_call x1, Pallas kernels, body(): pl.pallas_call(functools.partial(exchange_kernel, groups, rows, krylov_le...  28.2 us
    unnamed x8, local copies, waits for them, and re-layouts  4.56 us
    pallas_call x1, Pallas kernels, body(): pl.pallas_call(functools.partial(finish_kernel, rows_total, chunks), name...  4.06 us
    squeeze x1, local copies, waits for them, and re-layouts, body(): return (ritz_vectors, ritz_residuals, norms[0, :wanted_dev])  1.17 us

profile of v1, /device:TPU:0, one launch (start us, length us, event | category | flops | bytes accessed | tf_op | source)
XLA Modules:
  0.0 40.2 jit_solution(7614098215993624277)
XLA Ops:
  0.6 0.7 %bitcast_convert_fusion = f32[8,1]{0,1:T(1,128)S(1)} fusion(bf16[8]{0:T(256)(128)(2,1)} %param.7), kind=kLoop, calls=%fused_computation.2 | loop fusion | flops 8 | bytes 48 | tf_op jit(solution)/shard_map/broadcast_in_dim | solution.py:238
  1.3 0.1 pad.1.clone
  1.4 0.1 copy.7
  1.4 0.7 %convert_bitcast_fusion = f32[8,300]{1,0:T(8,128)S(1)} fusion(bf16[300,8]{0,1:T(8,128)(2,1)} %param.6), kind=kLoop, calls=%fused_computation.1 | loop fusion | flops 2400 | bytes 14400 | tf_op jit(solution)/shard_map/transpose | solution.py:236
  2.1 0.1 pad_maximum_fusion.packed_ref
  2.2 0.0 copy-start
  2.2 2.4 %copy-done = bf16[300,64,128]{2,1,0:T(8,128)(2,1)S(1)} copy-done((bf16[300,64,128]{2,1,0:T(8,128)(2,1)S(1)}, bf16[300,64,128]{2,1,0:T(8,128)(2,1)}, u32[]{:S(2)}) %copy-start) | copy-done | bytes 4915224
  4.6 28.2 %exchange.1 = (bf16[4,4,128,256]{3,2,1,0:T(8,128)(2,1)S(1)}, f32[4,8,128]{2,1,0:T(8,128)S(1)}, f32[8,128]{1,0:T(8,128)S(1)}) custom-call(f32[8,384]{1,0:T(8,128)S(1)} %pad_maximum_fusion.packed_ref, bf16[300,64,128]{2,1,0:T(8,128)(2,1)S(1)} %copy-done, bf16[300,64,128]{2,1,0:T(8,128)(2,1)} %image_ref.1), custom_call_target="tpu_custom_call" | custom-call | tf_op jit(solution)/shard_map/exchange/pallas_call | solution.py:247
  32.8 0.0 copy-start.1
  32.8 1.0 %copy-done.1 = bf16[4,4,128,256]{3,2,1,0:T(8,128)(2,1)} copy-done((bf16[4,4,128,256]{3,2,1,0:T(8,128)(2,1)}, bf16[4,4,128,256]{3,2,1,0:T(8,128)(2,1)S(1)}, u32[]{:S(2)}) %copy-start.1) | copy-done | bytes 1048600
  33.8 0.0 copy-start.2
  33.8 0.6 %copy-done.2 = f32[4,8,128]{2,1,0:T(8,128)} copy-done((f32[4,8,128]{2,1,0:T(8,128)}, f32[4,8,128]{2,1,0:T(8,128)S(1)}, u32[]{:S(2)}) %copy-start.2) | copy-done | bytes 16408
  34.4 0.0 copy-start.3
  34.4 0.6 %copy-done.3 = f32[8,128]{1,0:T(8,128)} copy-done((f32[8,128]{1,0:T(8,128)}, f32[8,128]{1,0:T(8,128)S(1)}, u32[]{:S(2)}) %copy-start.3) | copy-done | bytes 4120
  35.0 4.1 %finish.1 = (f32[8,64,512]{2,1,0:T(8,128)}, f32[8,64,512]{2,1,0:T(8,128)}, f32[1,128]{1,0:T(1,128)}) custom-call(bf16[4,4,128,256]{3,2,1,0:T(8,128)(2,1)} %copy-done.1, f32[4,8,128]{2,1,0:T(8,128)} %copy-done.2, f32[8,128]{1,0:T(8,128)} %copy-done.3), custom_call_target="tpu_custom_call" | custom-call | tf_op jit(solution)/shard_map/finish/pallas_call | solution.py:279
  39.0 1.2 %slice_bitcast_fusion = f32[8]{0:T(128)} fusion(f32[1,128]{1,0:T(1,128)} %get-tuple-element.14), kind=kLoop, calls=%fused_computation.3 | loop fusion | bytes 64 | tf_op jit(solution)/shard_map/squeeze | solution.py:299
  (1 shorter events, 0.0 us)
Async XLA Ops:
  2.2 2.4 %copy-start = (bf16[300,64,128]{2,1,0:T(8,128)(2,1)S(1)}, bf16[300,64,128]{2,1,0:T(8,128)(2,1)}, u32[]{:S(2)}) copy-start(bf16[300,64,128]{2,1,0:T(8,128)(2,1)} %basis_ref.1) | copy-start | bytes 14745604
  32.8 1.0 %copy-start.1 = (bf16[4,4,128,256]{3,2,1,0:T(8,128)(2,1)}, bf16[4,4,128,256]{3,2,1,0:T(8,128)(2,1)S(1)}, u32[]{:S(2)}) copy-start(bf16[4,4,128,256]{3,2,1,0:T(8,128)(2,1)S(1)} %get-tuple-element.9.coded_ref) | copy-start | bytes 3145732
  33.8 0.6 %copy-start.2 = (f32[4,8,128]{2,1,0:T(8,128)}, f32[4,8,128]{2,1,0:T(8,128)S(1)}, u32[]{:S(2)}) copy-start(f32[4,8,128]{2,1,0:T(8,128)S(1)} %get-tuple-element.10.stats_ref) | copy-start | bytes 49156
  34.4 0.6 %copy-start.3 = (f32[8,128]{1,0:T(8,128)}, f32[8,128]{1,0:T(8,128)S(1)}, u32[]{:S(2)}) copy-start(f32[8,128]{1,0:T(8,128)S(1)} %get-tuple-element.11.total_ref) | copy-start | bytes 12292

commit v2 on v1

--- a/solution.py
+++ b/solution.py
@@ -9,6 +9,7 @@
 from jax.sharding import PartitionSpec as P
 
 MESH = pl.DeviceIdType.MESH
+MIB = 1 << 20
 TILE = 16
 LANES = 128
 SPREAD = 256.0
@@ -31,9 +32,9 @@
 
 def exchange_kernel(
     groups, rows, krylov_len,
-    packed_ref, basis_ref, image_ref,
+    tridiag_ref, values_ref, basis_ref, image_ref,
     coded_ref, stats_ref, total_ref,
-    coefs, fields, spread, reps, expanded, coded, stat_send, stat_recv, row_send, row_recv,
+    packed_ref, coefs, fields, spread, reps, expanded, coded, stat_send, stat_recv, row_send, row_recv,
     load_sem, coef_sems, data_sems, own_sem, stat_sems, row_sems,
 ):
     wanted_dev, packed_width = packed_ref.shape
@@ -60,6 +61,12 @@
     for chunk in range(chunks):
         for copy in loads(chunk):
             copy.start()
+
+    near = grid_iota((wanted_dev, wanted_dev), 0) == grid_iota((wanted_dev, wanted_dev), 1)
+    own_values = jnp.broadcast_to(values_ref[...].astype(jnp.float32), (wanted_dev, wanted_dev))
+    own_values = jnp.sum(jnp.where(near, own_values, 0.0), axis=1, keepdims=True)
+    packed_ref[...] = jnp.broadcast_to(own_values, (wanted_dev, packed_width))
+    packed_ref[:, :krylov_len] = tridiag_ref[...].astype(jnp.float32)
 
     barrier = pltpu.get_barrier_semaphore()
     for step in range(1, groups):
@@ -219,7 +226,7 @@
             out_ref[:, :, source * inner_dev : (source + 1) * inner_dev] = size * expand_rows(scale, inner_dev)
     norms = jnp.broadcast_to(jnp.sqrt(resid_squares / ritz_squares), (wanted_dev, LANES))
     diagonal = lanes == grid_iota((wanted_dev, LANES), 0)
-    norm_ref[...] = jnp.sum(jnp.where(diagonal, norms, 0.0), axis=0, keepdims=True)
+    norm_ref[...] = jnp.sum(jnp.where(diagonal, norms, 0.0), axis=0)[:wanted_dev]
 
 
 def body(groups, rows, krylov_basis, krylov_image, tridiag_vectors, ritz_values):
@@ -231,18 +238,11 @@
     padded_len = cdiv(krylov_len, TILE) * TILE
     packed_width = cdiv(padded_len + 1, LANES) * LANES
     rows_total = float(outer_dev * inner_dev * groups * rows)
-    packed = jnp.concatenate(
-        [
-            tridiag_vectors.astype(jnp.float32).T,
-            jnp.zeros((wanted_dev, packed_width - krylov_len - 1), jnp.float32),
-            ritz_values.astype(jnp.float32)[:, None],
-        ],
-        axis=1,
-    )
     f32, bf16 = jnp.float32, jnp.bfloat16
     dma = pltpu.SemaphoreType.DMA
     anywhere = pl.BlockSpec(memory_space=pl.ANY)
     vmem = pl.BlockSpec(memory_space=pltpu.VMEM)
+    hbm = pl.BlockSpec(memory_space=pltpu.HBM)
     parts = cdiv(padded_len, LANES)
     coded, stats, total = pl.pallas_call(
         functools.partial(exchange_kernel, groups, rows, krylov_len),
@@ -252,9 +252,10 @@
             jax.ShapeDtypeStruct((groups, wanted_dev, LANES), f32),
             jax.ShapeDtypeStruct((wanted_dev, LANES), f32),
         ),
-        in_specs=[vmem, anywhere, anywhere],
+        in_specs=[vmem, vmem, hbm, hbm],
         out_specs=(anywhere, vmem, vmem),
         scratch_shapes=[
+            pltpu.VMEM((wanted_dev, packed_width), f32),
             pltpu.VMEM((groups, wanted_dev, packed_width), f32),
             pltpu.VMEM((2, chunks, padded_len, TILE, inner_dev), bf16),
             pltpu.VMEM((LANES, LANES * TILE), bf16),
@@ -273,9 +274,9 @@
             dma((2, rows)),
         ],
         compiler_params=pltpu.CompilerParams(
-            collective_id=0, has_side_effects=True, vmem_limit_bytes=48 * 1024 * 1024
+            collective_id=0, has_side_effects=True, vmem_limit_bytes=61 * MIB
         ),
-    )(packed, krylov_basis, krylov_image)
+    )(tridiag_vectors.T, ritz_values[None], krylov_basis, krylov_image)
     ritz_vectors, ritz_residuals, norms = pl.pallas_call(
         functools.partial(finish_kernel, rows_total, chunks),
         name="finish",
@@ -283,7 +284,7 @@
         out_shape=(
             jax.ShapeDtypeStruct((wanted_dev, outer_dev, groups * inner_dev), f32),
             jax.ShapeDtypeStruct((wanted_dev, outer_dev, groups * inner_dev), f32),
-            jax.ShapeDtypeStruct((1, LANES), f32),
+            jax.ShapeDtypeStruct((wanted_dev,), f32),
         ),
         in_specs=[
             pl.BlockSpec((groups, 1, block, 2 * inner_dev), lambda c: (0, c, 0, 0)),
@@ -293,10 +294,11 @@
         out_specs=(
             pl.BlockSpec((wanted_dev, TILE, groups * inner_dev), lambda c: (0, c, 0)),
             pl.BlockSpec((wanted_dev, TILE, groups * inner_dev), lambda c: (0, c, 0)),
-            pl.BlockSpec((1, LANES), lambda c: (0, 0)),
+            pl.BlockSpec((wanted_dev,), lambda c: (0,)),
         ),
+        compiler_params=pltpu.CompilerParams(vmem_limit_bytes=16 * MIB),
     )(coded, stats, total)
-    return ritz_vectors, ritz_residuals, norms[0, :wanted_dev]
+    return ritz_vectors, ritz_residuals, norms
 
 
 def solution(mesh):

time: 40.5 us -> 34.9 us (0.86)
  local copies, waits for them, and re-layouts: 5.89 us -> 2.62 us
  other arithmetic: 1.43 us -> 0 us
  Pallas kernels: 32.2 us -> 31.4 us
    unnamed x8 -> x6, local copies, waits for them, and re-layouts: 4.56 us -> 2.62 us
    pallas_call x1, Pallas kernels: 4.06 us -> 2.51 us  [body(): pl.pallas_call(functools.partial(finish_kernel, rows_total, chunks), name...]
    squeeze x1 -> x0, local copies, waits for them, and re-layouts: 1.17 us -> none  [body(): return (ritz_vectors, ritz_residuals, norms[0, :wanted_dev])]
    transpose x1 -> x0, other arithmetic: 0.69 us -> none  [body(): tridiag_vectors.astype(jnp.float32)]
    pallas_call x1, Pallas kernels: 28.2 us -> 28.8 us  [body(): pl.pallas_call(functools.partial(exchange_kernel, groups, rows, krylov_le...]
    broadcast_in_dim x1 -> x0, other arithmetic: 0.66 us -> none  [body(): ritz_values.astype(jnp.float32)[:, None]]
where the time goes in v2:
time: 34.9 us; the launch traced here: 34.6 us
  Pallas kernels  31.4 us (90%)
  local copies, waits for them, and re-layouts  2.62 us (8%)
  between operations  0.65 us (2%)
    pallas_call x1, Pallas kernels, body(): pl.pallas_call(functools.partial(exchange_kernel, groups, rows, krylov_le...  28.8 us
    unnamed x6, local copies, waits for them, and re-layouts  2.62 us
    pallas_call x1, Pallas kernels, body(): pl.pallas_call(functools.partial(finish_kernel, rows_total, chunks), name...  2.51 us

profile of v2, /device:TPU:0, one launch (start us, length us, event | category | flops | bytes accessed | tf_op | source)
XLA Modules:
  0.0 34.6 jit_solution(18054972868145009600)
XLA Ops:
  0.6 28.8 %exchange.1 = (bf16[4,4,128,256]{3,2,1,0:T(8,128)(2,1)}, f32[4,8,128]{2,1,0:T(8,128)}, f32[8,128]{1,0:T(8,128)}) custom-call(bf16[8,300]{1,0:T(8,128)(2,1)} %bitcast.2, bf16[1,8]{1,0:T(2,128)(2,1)} %bitcast.3, bf16[300,64,128]{2,1,0:T(8,128)(2,1)} %basis_ref.1, bf16[300,64,128]{2,1,0:T(8,128)(2,1)} %image_ref.1), custom_call_target="tpu_custom_call" | custom-call | tf_op jit(solution)/shard_map/exchange/pallas_call | solution.py:247
  29.5 0.0 copy-start
  29.5 1.2 %copy-done = bf16[4,4,128,256]{3,2,1,0:T(8,128)(2,1)S(1)} copy-done((bf16[4,4,128,256]{3,2,1,0:T(8,128)(2,1)S(1)}, bf16[4,4,128,256]{3,2,1,0:T(8,128)(2,1)}, u32[]{:S(2)}) %copy-start) | copy-done | bytes 1048600
  30.7 0.0 copy-start.1
  30.7 0.7 %copy-done.1 = f32[4,8,128]{2,1,0:T(8,128)S(1)} copy-done((f32[4,8,128]{2,1,0:T(8,128)S(1)}, f32[4,8,128]{2,1,0:T(8,128)}, u32[]{:S(2)}) %copy-start.1) | copy-done | bytes 16408
  31.4 0.0 copy-start.2
  31.4 0.7 %copy-done.2 = f32[8,128]{1,0:T(8,128)S(1)} copy-done((f32[8,128]{1,0:T(8,128)S(1)}, f32[8,128]{1,0:T(8,128)}, u32[]{:S(2)}) %copy-start.2) | copy-done | bytes 4120
  32.1 2.5 %finish.1 = (f32[8,64,512]{2,1,0:T(8,128)}, f32[8,64,512]{2,1,0:T(8,128)}, f32[8]{0:T(128)}) custom-call(bf16[4,4,128,256]{3,2,1,0:T(8,128)(2,1)S(1)} %copy-done, f32[4,8,128]{2,1,0:T(8,128)S(1)} %copy-done.1, f32[8,128]{1,0:T(8,128)S(1)} %copy-done.2), custom_call_target="tpu_custom_call" | custom-call | tf_op jit(solution)/shard_map/finish/pallas_call | solution.py:280
Async XLA Ops:
  29.5 1.2 %copy-start = (bf16[4,4,128,256]{3,2,1,0:T(8,128)(2,1)S(1)}, bf16[4,4,128,256]{3,2,1,0:T(8,128)(2,1)}, u32[]{:S(2)}) copy-start(bf16[4,4,128,256]{3,2,1,0:T(8,128)(2,1)} %get-tuple-element.6.coded_ref) | copy-start | bytes 3145732
  30.7 0.7 %copy-start.1 = (f32[4,8,128]{2,1,0:T(8,128)S(1)}, f32[4,8,128]{2,1,0:T(8,128)}, u32[]{:S(2)}) copy-start(f32[4,8,128]{2,1,0:T(8,128)} %get-tuple-element.7.stats_ref) | copy-start | bytes 49156
  31.4 0.7 %copy-start.2 = (f32[8,128]{1,0:T(8,128)S(1)}, f32[8,128]{1,0:T(8,128)}, u32[]{:S(2)}) copy-start(f32[8,128]{1,0:T(8,128)} %get-tuple-element.8.total_ref) | copy-start | bytes 12292

commit v3 on v2

--- a/solution.py
+++ b/solution.py
@@ -10,7 +10,8 @@
 
 MESH = pl.DeviceIdType.MESH
 MIB = 1 << 20
-TILE = 16
+TILE = 8
+STEP = 16
 LANES = 128
 SPREAD = 256.0
 REACH = 86.0
@@ -34,16 +35,16 @@
     groups, rows, krylov_len,
     tridiag_ref, values_ref, basis_ref, image_ref,
     coded_ref, stats_ref, total_ref,
-    packed_ref, coefs, fields, spread, reps, expanded, coded, stat_send, stat_recv, row_send, row_recv,
-    load_sem, coef_sems, data_sems, own_sem, stat_sems, row_sems,
+    packed_ref, coefs, fields, spread, reps, expanded, coded, stat_send, stat_recv, square_send, square_recv,
+    load_sem, coef_sems, data_sems, own_sem, stat_sems, square_sems,
 ):
     wanted_dev, packed_width = packed_ref.shape
     wanted = groups * wanted_dev
     chunks = fields.shape[1]
     inner_dev = basis_ref.shape[2]
     padded_len = fields.shape[2]
-    steps = padded_len // TILE
-    wide = TILE * TILE
+    steps = padded_len // STEP
+    wide = STEP * TILE
     block = wanted_dev * TILE
     grp = lax.axis_index("grp")
     row = lax.axis_index("row")
@@ -69,25 +70,32 @@
     packed_ref[:, :krylov_len] = tridiag_ref[...].astype(jnp.float32)
 
     barrier = pltpu.get_barrier_semaphore()
-    for step in range(1, groups):
-        pl.semaphore_signal(barrier, inc=1, device_id={"grp": lax.rem(grp + step, groups)}, device_id_type=MESH)
-    for step in range(1, rows):
-        pl.semaphore_signal(barrier, inc=1, device_id={"row": lax.rem(row + step, rows)}, device_id_type=MESH)
-    pl.semaphore_wait(barrier, groups + rows - 2)
-
-    def remote(src, dst, sems, index, axis, step):
-        me, size = (grp, groups) if axis == "grp" else (row, rows)
+    def others(action):
+        for across in range(groups):
+            lax.fori_loop(1 if across == 0 else 0, rows, functools.partial(action, across), 0)
+
+    def device(across, along):
+        return {"grp": lax.rem(grp + across, groups), "row": lax.rem(row + along, rows)}
+
+    def greet(across, along, carry):
+        pl.semaphore_signal(barrier, inc=1, device_id=device(across, along), device_id_type=MESH)
+        return carry
+
+    others(greet)
+    pl.semaphore_wait(barrier, groups * rows - 1)
+
+    def remote(src, dst, sems, index, across, along=0):
         return pltpu.make_async_remote_copy(
             src_ref=src,
             dst_ref=dst,
             send_sem=sems.at[(0,) + index],
             recv_sem=sems.at[(1,) + index],
-            device_id={axis: lax.rem(me + step, size)},
+            device_id=device(across, along),
             device_id_type=MESH,
         )
 
     def coef_copy(step):
-        return remote(packed_ref, coefs.at[grp], coef_sems, (step,), "grp", step)
+        return remote(packed_ref, coefs.at[grp], coef_sems, (step,), step)
 
     for step in range(1, groups):
         coef_copy(step).start()
@@ -101,7 +109,7 @@
                 )
     shape = spread.shape
     spread[...] = jnp.where(
-        lax.shift_right_logical(grid_iota(shape, 1), 4) == grid_iota(shape, 0), 1.0, 0.0
+        lax.shift_right_logical(grid_iota(shape, 1), 3) == grid_iota(shape, 0), 1.0, 0.0
     ).astype(jnp.bfloat16)
 
     for step in range(1, groups):
@@ -109,13 +117,13 @@
 
     all_coefs = coefs[...].reshape(wanted, packed_width)
     shift_values = expand_rows(all_coefs[:, packed_width - 1 :], inner_dev)
-    for part in range(cdiv(steps * TILE, LANES)):
+    for part in range(cdiv(padded_len, LANES)):
         reps[part] = jnp.dot(
             all_coefs[:, part * LANES : (part + 1) * LANES].astype(jnp.bfloat16),
             spread[...],
             preferred_element_type=jnp.float32,
         )
-    per_part = LANES // TILE
+    per_part = LANES // STEP
     same = (grid_iota((TILE, wide), 1) & (TILE - 1)) == grid_iota((TILE, wide), 0)
     for step in range(steps):
         at = (step % per_part) * wide
@@ -128,7 +136,7 @@
         return remote(
             coded.at[chunk, pl.ds(pl.multiple_of(dest * block, block), block)],
             coded_ref.at[grp, chunk],
-            data_sems, (chunk, step), "grp", step,
+            data_sems, (chunk, step), step,
         )
 
     def own_copy(chunk):
@@ -140,10 +148,27 @@
 
     def stat_copy(step):
         return remote(
-            stat_send.at[lax.rem(grp + step, groups)], stat_recv.at[grp], stat_sems, (step,), "grp", step
-        )
-
-    def compute(chunk, stats):
+            stat_send.at[lax.rem(grp + step, groups)], stat_recv.at[grp], stat_sems, (step,), step
+        )
+
+    def square_copy(across, along):
+        return remote(
+            square_send.at[lax.rem(grp + across, groups)], square_recv.at[grp * rows + row],
+            square_sems, (across, along), across, along,
+        )
+
+    def square_start(across, along, carry):
+        square_copy(across, along).start()
+        return carry
+
+    def square_wait(across, along, carry):
+        square_copy(across, along).wait()
+        return carry
+
+    column = grid_iota((wanted, LANES), 0) % wanted_dev
+
+    def compute(chunk, carry):
+        stats, sums = carry
         for copy in loads(chunk):
             copy.wait()
         both = jnp.concatenate(
@@ -163,10 +188,12 @@
                 wanted * TILE, inner_dev
             ).astype(jnp.bfloat16)
             stats = jnp.where(lane_stats == 2 * chunk + kind, most, stats)
-            stats = jnp.where(lane_stats == 2 * chunks + kind, stats + squares, stats)
+            sums = jnp.where(lane_stats == column + kind * wanted_dev, sums + squares, sums)
 
         @pl.when(chunk == chunks - 1)
         def _():
+            square_send[...] = jnp.sum(sums.reshape(groups, wanted_dev, LANES), axis=1, keepdims=True)
+            others(square_start)
             stat_send[...] = stats.reshape(groups, wanted_dev, LANES)
             for step in range(1, groups):
                 stat_copy(step).start()
@@ -174,25 +201,18 @@
         for step in range(1, groups):
             data_copy(chunk, step).start()
         own_copy(chunk).start()
-        return stats
-
-    lax.fori_loop(0, chunks, compute, jnp.zeros((wanted, LANES), jnp.float32))
+        return stats, sums
+
+    nothing = jnp.zeros((wanted, LANES), jnp.float32)
+    lax.fori_loop(0, chunks, compute, (nothing, nothing))
 
     for step in range(1, groups):
         stat_copy(step).wait()
     stat_recv[grp] = stat_send[grp]
-    row_send[...] = jnp.sum(stat_recv[...], axis=0)
-
-    def row_copy(step):
-        return remote(row_send, row_recv.at[row], row_sems, (step,), "row", step)
-
-    for step in range(1, rows):
-        row_copy(step).start()
     stats_ref[...] = stat_recv[...]
-    row_recv[row] = row_send[...]
-    for step in range(1, rows):
-        row_copy(step).wait()
-    total_ref[...] = jnp.sum(row_recv[...], axis=0)
+    others(square_wait)
+    square_recv[grp * rows + row] = square_send[grp]
+    total_ref[...] = jnp.sum(square_recv[...], axis=0)
 
     def finish(chunk, carry):
         for step in range(1, groups):
@@ -203,30 +223,32 @@
     lax.fori_loop(0, chunks, finish, 0)
 
 
-def finish_kernel(rows_total, chunks, coded_ref, stats_ref, total_ref, ritz_ref, resid_ref, norm_ref):
-    chunk = pl.program_id(0)
+def finish_kernel(rows_total, coded_ref, stats_ref, total_ref, ritz_ref, resid_ref, norm_ref):
     groups, wanted_dev = stats_ref.shape[:2]
+    several = coded_ref.shape[1]
+    first = pl.program_id(0) * several
     inner_dev = coded_ref.shape[3] // 2
     lanes = grid_iota((wanted_dev, LANES), 1)
+    columns = grid_iota((wanted_dev, LANES), 0)
 
     def pick(tile, lane):
         return jnp.sum(jnp.where(lanes == lane, tile, 0.0), axis=1, keepdims=True)
 
-    total = total_ref[...]
-    ritz_squares = pick(total, 2 * chunks) + 1.0
-    resid_squares = pick(total, 2 * chunks + 1)
+    total = jnp.broadcast_to(total_ref[...], (wanted_dev, LANES))
+    ritz_squares = pick(total, columns) + 1.0
+    resid_squares = pick(total, columns + wanted_dev)
     factor = jnp.sqrt(rows_total / ritz_squares)
     for source in range(groups):
-        for kind, out_ref in enumerate((ritz_ref, resid_ref)):
-            scale = pick(stats_ref[source], 2 * chunk + kind) * (factor * (1.0 / SPREAD))
-            codes = coded_ref[source, 0, :, kind * inner_dev : (kind + 1) * inner_dev].astype(jnp.float32)
-            size = jnp.exp((jnp.log(jnp.abs(codes)) + REACH) * (1.0 / SLOPE)) - 1.0
-            size = jnp.where(codes < 0.0, -size, size)
-            size = size.reshape(wanted_dev, TILE, inner_dev)
-            out_ref[:, :, source * inner_dev : (source + 1) * inner_dev] = size * expand_rows(scale, inner_dev)
+        for part in range(several):
+            for kind, out_ref in enumerate((ritz_ref, resid_ref)):
+                scale = pick(stats_ref[source], 2 * (first + part) + kind) * (factor * (1.0 / SPREAD))
+                codes = coded_ref[source, part, :, kind * inner_dev : (kind + 1) * inner_dev].astype(jnp.float32)
+                size = jnp.exp((jnp.log(jnp.abs(codes)) + REACH) * (1.0 / SLOPE)) - 1.0
+                size = jnp.where(codes < 0.0, -size, size)
+                size = size.reshape(wanted_dev, TILE, inner_dev) * expand_rows(scale, inner_dev)
+                out_ref[:, part * TILE : (part + 1) * TILE, source * inner_dev : (source + 1) * inner_dev] = size
     norms = jnp.broadcast_to(jnp.sqrt(resid_squares / ritz_squares), (wanted_dev, LANES))
-    diagonal = lanes == grid_iota((wanted_dev, LANES), 0)
-    norm_ref[...] = jnp.sum(jnp.where(diagonal, norms, 0.0), axis=0)[:wanted_dev]
+    norm_ref[...] = jnp.sum(jnp.where(lanes == columns, norms, 0.0), axis=0)[:wanted_dev]
 
 
 def body(groups, rows, krylov_basis, krylov_image, tridiag_vectors, ritz_values):
@@ -235,7 +257,7 @@
     wanted = groups * wanted_dev
     chunks = outer_dev // TILE
     block = wanted_dev * TILE
-    padded_len = cdiv(krylov_len, TILE) * TILE
+    padded_len = cdiv(krylov_len, STEP) * STEP
     packed_width = cdiv(padded_len + 1, LANES) * LANES
     rows_total = float(outer_dev * inner_dev * groups * rows)
     f32, bf16 = jnp.float32, jnp.bfloat16
@@ -244,13 +266,14 @@
     vmem = pl.BlockSpec(memory_space=pltpu.VMEM)
     hbm = pl.BlockSpec(memory_space=pltpu.HBM)
     parts = cdiv(padded_len, LANES)
+    several = 2 if chunks % 2 == 0 else 1
     coded, stats, total = pl.pallas_call(
         functools.partial(exchange_kernel, groups, rows, krylov_len),
         name="exchange",
         out_shape=(
             jax.ShapeDtypeStruct((groups, chunks, block, 2 * inner_dev), bf16),
             jax.ShapeDtypeStruct((groups, wanted_dev, LANES), f32),
-            jax.ShapeDtypeStruct((wanted_dev, LANES), f32),
+            jax.ShapeDtypeStruct((1, LANES), f32),
         ),
         in_specs=[vmem, vmem, hbm, hbm],
         out_specs=(anywhere, vmem, vmem),
@@ -264,36 +287,36 @@
             pltpu.VMEM((chunks, wanted * TILE, 2 * inner_dev), bf16),
             pltpu.VMEM((groups, wanted_dev, LANES), f32),
             pltpu.VMEM((groups, wanted_dev, LANES), f32),
-            pltpu.VMEM((wanted_dev, LANES), f32),
-            pltpu.VMEM((rows, wanted_dev, LANES), f32),
+            pltpu.VMEM((groups, 1, LANES), f32),
+            pltpu.VMEM((groups * rows, 1, LANES), f32),
             dma((2, chunks)),
             dma((2, groups)),
             dma((2, chunks, groups)),
             dma((chunks,)),
             dma((2, groups)),
-            dma((2, rows)),
+            dma((2, groups, rows)),
         ],
         compiler_params=pltpu.CompilerParams(
-            collective_id=0, has_side_effects=True, vmem_limit_bytes=61 * MIB
+            collective_id=0, has_side_effects=True, vmem_limit_bytes=60 * MIB
         ),
     )(tridiag_vectors.T, ritz_values[None], krylov_basis, krylov_image)
     ritz_vectors, ritz_residuals, norms = pl.pallas_call(
-        functools.partial(finish_kernel, rows_total, chunks),
+        functools.partial(finish_kernel, rows_total),
         name="finish",
-        grid=(chunks,),
+        grid=(chunks // several,),
         out_shape=(
             jax.ShapeDtypeStruct((wanted_dev, outer_dev, groups * inner_dev), f32),
             jax.ShapeDtypeStruct((wanted_dev, outer_dev, groups * inner_dev), f32),
             jax.ShapeDtypeStruct((wanted_dev,), f32),
         ),
         in_specs=[
-            pl.BlockSpec((groups, 1, block, 2 * inner_dev), lambda c: (0, c, 0, 0)),
+            pl.BlockSpec((groups, several, block, 2 * inner_dev), lambda c: (0, c, 0, 0)),
             pl.BlockSpec((groups, wanted_dev, LANES), lambda c: (0, 0, 0)),
-            pl.BlockSpec((wanted_dev, LANES), lambda c: (0, 0)),
+            pl.BlockSpec((1, LANES), lambda c: (0, 0)),
         ],
         out_specs=(
-            pl.BlockSpec((wanted_dev, TILE, groups * inner_dev), lambda c: (0, c, 0)),
-            pl.BlockSpec((wanted_dev, TILE, groups * inner_dev), lambda c: (0, c, 0)),
+            pl.BlockSpec((wanted_dev, several * TILE, groups * inner_dev), lambda c: (0, c, 0)),
+            pl.BlockSpec((wanted_dev, several * TILE, groups * inner_dev), lambda c: (0, c, 0)),
             pl.BlockSpec((wanted_dev,), lambda c: (0,)),
         ),
         compiler_params=pltpu.CompilerParams(vmem_limit_bytes=16 * MIB),

time: 34.9 us -> 33.6 us (0.963)
  Pallas kernels: 31.4 us -> 30 us
    pallas_call x1, Pallas kernels: 28.8 us -> 27.5 us  [body(): pl.pallas_call(functools.partial(exchange_kernel, groups, rows, krylov_le...]
where the time goes in v3:
time: 33.6 us; the launch traced here: 33.3 us
  Pallas kernels  30 us (89%)
  local copies, waits for them, and re-layouts  2.6 us (8%)
  between operations  0.65 us (2%)
    pallas_call x1, Pallas kernels, body(): pl.pallas_call(functools.partial(exchange_kernel, groups, rows, krylov_le...  27.5 us
    unnamed x6, local copies, waits for them, and re-layouts  2.6 us
    pallas_call x1, Pallas kernels, body(): pl.pallas_call(functools.partial(finish_kernel, rows_total), name='finish...  2.51 us

profile of v3, /device:TPU:0, one launch (start us, length us, event | category | flops | bytes accessed | tf_op | source)
XLA Modules:
  0.0 33.3 jit_solution(123957375815713000)
XLA Ops:
  0.6 27.5 %exchange.1 = (bf16[4,8,64,256]{3,2,1,0:T(8,128)(2,1)}, f32[4,8,128]{2,1,0:T(8,128)}, f32[1,128]{1,0:T(1,128)}) custom-call(bf16[8,300]{1,0:T(8,128)(2,1)} %bitcast.2, bf16[1,8]{1,0:T(2,128)(2,1)} %bitcast.3, bf16[300,64,128]{2,1,0:T(8,128)(2,1)} %basis_ref.1, bf16[300,64,128]{2,1,0:T(8,128)(2,1)} %image_ref.1), custom_call_target="tpu_custom_call" | custom-call | tf_op jit(solution)/shard_map/exchange/pallas_call | solution.py:270
  28.1 0.0 copy-start
  28.2 1.2 %copy-done = bf16[4,8,64,256]{3,2,1,0:T(8,128)(2,1)S(1)} copy-done((bf16[4,8,64,256]{3,2,1,0:T(8,128)(2,1)S(1)}, bf16[4,8,64,256]{3,2,1,0:T(8,128)(2,1)}, u32[]{:S(2)}) %copy-start) | copy-done | bytes 1048600
  29.4 0.0 copy-start.1
  29.4 0.7 %copy-done.1 = f32[4,8,128]{2,1,0:T(8,128)S(1)} copy-done((f32[4,8,128]{2,1,0:T(8,128)S(1)}, f32[4,8,128]{2,1,0:T(8,128)}, u32[]{:S(2)}) %copy-start.1) | copy-done | bytes 16408
  30.1 0.0 copy-start.2
  30.1 0.7 %copy-done.2 = f32[1,128]{1,0:T(1,128)S(1)} copy-done((f32[1,128]{1,0:T(1,128)S(1)}, f32[1,128]{1,0:T(1,128)}, u32[]{:S(2)}) %copy-start.2) | copy-done | bytes 536
  30.8 2.5 %finish.1 = (f32[8,64,512]{2,1,0:T(8,128)}, f32[8,64,512]{2,1,0:T(8,128)}, f32[8]{0:T(128)}) custom-call(bf16[4,8,64,256]{3,2,1,0:T(8,128)(2,1)S(1)} %copy-done, f32[4,8,128]{2,1,0:T(8,128)S(1)} %copy-done.1, f32[1,128]{1,0:T(1,128)S(1)} %copy-done.2), custom_call_target="tpu_custom_call" | custom-call | tf_op jit(solution)/shard_map/finish/pallas_call | solution.py:303
Async XLA Ops:
  28.1 1.2 %copy-start = (bf16[4,8,64,256]{3,2,1,0:T(8,128)(2,1)S(1)}, bf16[4,8,64,256]{3,2,1,0:T(8,128)(2,1)}, u32[]{:S(2)}) copy-start(bf16[4,8,64,256]{3,2,1,0:T(8,128)(2,1)} %get-tuple-element.6.coded_ref) | copy-start | bytes 3145732
  29.4 0.7 %copy-start.1 = (f32[4,8,128]{2,1,0:T(8,128)S(1)}, f32[4,8,128]{2,1,0:T(8,128)}, u32[]{:S(2)}) copy-start(f32[4,8,128]{2,1,0:T(8,128)} %get-tuple-element.7.stats_ref) | copy-start | bytes 49156
  30.1 0.7 %copy-start.2 = (f32[1,128]{1,0:T(1,128)S(1)}, f32[1,128]{1,0:T(1,128)}, u32[]{:S(2)}) copy-start(f32[1,128]{1,0:T(1,128)} %get-tuple-element.8.total_ref) | copy-start | bytes 1540

commit v4 on v3

--- a/solution.py
+++ b/solution.py
@@ -297,7 +297,7 @@
             dma((2, groups, rows)),
         ],
         compiler_params=pltpu.CompilerParams(
-            collective_id=0, has_side_effects=True, vmem_limit_bytes=60 * MIB
+            collective_id=0, has_side_effects=True, vmem_limit_bytes=52 * MIB
         ),
     )(tridiag_vectors.T, ritz_values[None], krylov_basis, krylov_image)
     ritz_vectors, ritz_residuals, norms = pl.pallas_call(

time: 33.6 us -> 30.8 us (0.917)
  Pallas kernels: 30 us -> 28.6 us
  local copies, waits for them, and re-layouts: 2.6 us -> 1.34 us
    pallas_call x1, Pallas kernels: 27.5 us -> 26.1 us  [body(): pl.pallas_call(functools.partial(exchange_kernel, groups, rows, krylov_le...]
    unnamed x6 -> x4, local copies, waits for them, and re-layouts: 2.6 us -> 1.34 us
where the time goes in v4:
time: 30.8 us; the launch traced here: 30.6 us
  Pallas kernels  28.6 us (93%)
  local copies, waits for them, and re-layouts  1.34 us (4%)
  between operations  0.65 us (2%)
    pallas_call x1, Pallas kernels, body(): pl.pallas_call(functools.partial(exchange_kernel, groups, rows, krylov_le...  26.1 us
    pallas_call x1, Pallas kernels, body(): pl.pallas_call(functools.partial(finish_kernel, rows_total), name='finish...  2.52 us
    unnamed x4, local copies, waits for them, and re-layouts  1.34 us

profile of v4, /device:TPU:0, one launch (start us, length us, event | category | flops | bytes accessed | tf_op | source)
XLA Modules:
  0.0 30.6 jit_solution(561791253926207398)
XLA Ops:
  0.6 0.0 copy-start
  0.6 0.7 %copy-done = bf16[300,8]{0,1:T(8,128)(2,1)S(1)} copy-done((bf16[300,8]{0,1:T(8,128)(2,1)S(1)}, bf16[300,8]{0,1:T(8,128)(2,1)}, u32[]{:S(2)}) %copy-start) | copy-done | bytes 4824
  1.3 0.0 copy-start.1
  1.3 0.7 %copy-done.1 = bf16[8]{0:T(256)(128)(2,1)S(1)} copy-done((bf16[8]{0:T(256)(128)(2,1)S(1)}, bf16[8]{0:T(256)(128)(2,1)}, u32[]{:S(2)}) %copy-start.1) | copy-done | bytes 40
  2.0 26.1 %exchange.1 = (bf16[4,8,64,256]{3,2,1,0:T(8,128)(2,1)S(1)}, f32[4,8,128]{2,1,0:T(8,128)S(1)}, f32[1,128]{1,0:T(1,128)S(1)}) custom-call(bf16[8,300]{1,0:T(8,128)(2,1)S(1)} %bitcast.2, bf16[1,8]{1,0:T(2,128)(2,1)S(1)} %bitcast.3, bf16[300,64,128]{2,1,0:T(8,128)(2,1)} %basis_ref.1, bf16[300,64,128]{2,1,0:T(8,128)(2,1)} %image_ref.1), custom_call_target="tpu_custom_call" | custom-call | tf_op jit(solution)/shard_map/exchange/pallas_call | solution.py:270
  28.1 2.5 %finish.1 = (f32[8,64,512]{2,1,0:T(8,128)}, f32[8,64,512]{2,1,0:T(8,128)}, f32[8]{0:T(128)}) custom-call(bf16[4,8,64,256]{3,2,1,0:T(8,128)(2,1)S(1)} %get-tuple-element.6.coded_ref, f32[4,8,128]{2,1,0:T(8,128)S(1)} %get-tuple-element.7.stats_ref, f32[1,128]{1,0:T(1,128)S(1)} %get-tuple-element.8.total_ref), custom_call_target="tpu_custom_call" | custom-call | tf_op jit(solution)/shard_map/finish/pallas_call | solution.py:303
Async XLA Ops:
  0.6 0.7 %copy-start = (bf16[300,8]{0,1:T(8,128)(2,1)S(1)}, bf16[300,8]{0,1:T(8,128)(2,1)}, u32[]{:S(2)}) copy-start(bf16[300,8]{0,1:T(8,128)(2,1)} %param.6) | copy-start | bytes 14404
  1.3 0.7 %copy-start.1 = (bf16[8]{0:T(256)(128)(2,1)S(1)}, bf16[8]{0:T(256)(128)(2,1)}, u32[]{:S(2)}) copy-start(bf16[8]{0:T(256)(128)(2,1)} %param.7) | copy-start | bytes 52

commit v5 on v4

--- a/solution.py
+++ b/solution.py
@@ -266,7 +266,7 @@
     vmem = pl.BlockSpec(memory_space=pltpu.VMEM)
     hbm = pl.BlockSpec(memory_space=pltpu.HBM)
     parts = cdiv(padded_len, LANES)
-    several = 2 if chunks % 2 == 0 else 1
+    several = math.gcd(chunks, 4)
     coded, stats, total = pl.pallas_call(
         functools.partial(exchange_kernel, groups, rows, krylov_len),
         name="exchange",

time: 30.8 us -> 30.5 us (level)
    pallas_call x1, Pallas kernels: 2.52 us -> 2.14 us  [body(): pl.pallas_call(functools.partial(finish_kernel, rows_total), name='finish...]
where the time goes in v5:
time: 30.5 us; the launch traced here: 30.3 us
  Pallas kernels  28.3 us (93%)
  local copies, waits for them, and re-layouts  1.34 us (4%)
  between operations  0.65 us (2%)
    pallas_call x1, Pallas kernels, body(): pl.pallas_call(functools.partial(exchange_kernel, groups, rows, krylov_le...  26.1 us
    pallas_call x1, Pallas kernels, body(): pl.pallas_call(functools.partial(finish_kernel, rows_total), name='finish...  2.14 us
    unnamed x4, local copies, waits for them, and re-layouts  1.34 us

profile of v5, /device:TPU:0, one launch (start us, length us, event | category | flops | bytes accessed | tf_op | source)
XLA Modules:
  0.0 30.3 jit_solution(8460399461764404166)
XLA Ops:
  0.6 0.0 copy-start
  0.6 0.7 %copy-done = bf16[300,8]{0,1:T(8,128)(2,1)S(1)} copy-done((bf16[300,8]{0,1:T(8,128)(2,1)S(1)}, bf16[300,8]{0,1:T(8,128)(2,1)}, u32[]{:S(2)}) %copy-start) | copy-done | bytes 4824
  1.3 0.0 copy-start.1
  1.3 0.7 %copy-done.1 = bf16[8]{0:T(256)(128)(2,1)S(1)} copy-done((bf16[8]{0:T(256)(128)(2,1)S(1)}, bf16[8]{0:T(256)(128)(2,1)}, u32[]{:S(2)}) %copy-start.1) | copy-done | bytes 40
  2.0 26.1 %exchange.1 = (bf16[4,8,64,256]{3,2,1,0:T(8,128)(2,1)S(1)}, f32[4,8,128]{2,1,0:T(8,128)S(1)}, f32[1,128]{1,0:T(1,128)S(1)}) custom-call(bf16[8,300]{1,0:T(8,128)(2,1)S(1)} %bitcast.2, bf16[1,8]{1,0:T(2,128)(2,1)S(1)} %bitcast.3, bf16[300,64,128]{2,1,0:T(8,128)(2,1)} %basis_ref.1, bf16[300,64,128]{2,1,0:T(8,128)(2,1)} %image_ref.1), custom_call_target="tpu_custom_call" | custom-call | tf_op jit(solution)/shard_map/exchange/pallas_call | solution.py:270
  28.1 2.1 %finish.1 = (f32[8,64,512]{2,1,0:T(8,128)}, f32[8,64,512]{2,1,0:T(8,128)}, f32[8]{0:T(128)}) custom-call(bf16[4,8,64,256]{3,2,1,0:T(8,128)(2,1)S(1)} %get-tuple-element.6.coded_ref, f32[4,8,128]{2,1,0:T(8,128)S(1)} %get-tuple-element.7.stats_ref, f32[1,128]{1,0:T(1,128)S(1)} %get-tuple-element.8.total_ref), custom_call_target="tpu_custom_call" | custom-call | tf_op jit(solution)/shard_map/finish/pallas_call | solution.py:303
Async XLA Ops:
  0.6 0.7 %copy-start = (bf16[300,8]{0,1:T(8,128)(2,1)S(1)}, bf16[300,8]{0,1:T(8,128)(2,1)}, u32[]{:S(2)}) copy-start(bf16[300,8]{0,1:T(8,128)(2,1)} %param.6) | copy-start | bytes 14404
  1.3 0.7 %copy-start.1 = (bf16[8]{0:T(256)(128)(2,1)S(1)}, bf16[8]{0:T(256)(128)(2,1)}, u32[]{:S(2)}) copy-start(bf16[8]{0:T(256)(128)(2,1)} %param.7) | copy-start | bytes 52
